TPU v7x, 256 devices: a whole 4x4x8 slice. The times are simulated.
256 devices in a mesh: lon: 16 (over x, y_hi, core), lat: 16 (over y_lo, z).
Axes of the slice: x: 4, y: 4 (y_hi: 2, y_lo: 2; y = y_hi * 2 + y_lo), z: 8, core: 2. Of those that a mesh axis runs over, the one named last changes fastest.
Arguments:
- grid_latent: bfloat16 [16, 16, 1024, 512], P('lat', 'lon'), may hold values from -6 to 6
- mesh_latent: bfloat16 [16, 16, 160, 512], P('lat', 'lon'), may hold values from -6 to 6
- edge_geometry: float32 [16, 16, 4, 2048], P('lat', 'lon'), may hold values from -6 to 6
- senders: int32 [16, 16, 2048], P('lat', 'lon'), may hold values from 0 to 1023
- receivers: int32 [16, 16, 2048], P('lat', 'lon'), may hold values from 0 to 1439, as said below
- w_grid: bfloat16 [512, 512], replicated, may hold values from -0.25 to 0.25
- w_mesh: bfloat16 [512, 512], replicated, may hold values from -0.25 to 0.25
- w_edge: float32 [4, 512], replicated, may hold values from -3 to 3
- edge_bias: float32 [512], replicated, may hold values from -3 to 3
- w_message: bfloat16 [512, 512], replicated, may hold values from -0.25 to 0.25
- w_node: bfloat16 [1024, 512], replicated, may hold values from -0.1875 to 0.1875
- w_output: bfloat16 [512, 512], replicated, may hold values from -0.25 to 0.25
- norm_gain: float32 [512], replicated, may hold values from 0.1 to 1.9
- norm_bias: float32 [512], replicated, may hold values from -3 to 3
Outputs:
- mesh_out: bfloat16 [16, 16, 160, 512], P('lat', 'lon')
Inputs may be any that keep to these rules, and one draw needn't show every extreme that they name: `receivers`: r // 160 is a neighbour slot s from 0 to 8 (latitude offset s // 3 - 1, longitude offset s % 3 - 1); edges of the first band never name latitude offset -1, those of the last band never +1. For s other than 4, with k = s for s < 4 and k = s - 1 otherwise, the row r % 160 lies in k * 16 to k * 16 + 15 for s = 1, 3, 5, 7 and in k * 16 to k * 16 + 3 for s = 0, 2, 6, 8.
All inputs are finite; a program needn't handle non-finite values.
Results may differ from a plain program's by a relative error of at most 0.0095.
Values may be sent and summed in bfloat16 or wider, within the bound.
A program may use at most 64 MiB of HBM per device.

v0:
```python
import jax
import jax.numpy as jnp
from jax import lax
from jax.sharding import PartitionSpec as P

B_SIDE = 16


border_slots = (0, 1, 2, 3, 5, 6, 7, 8)


def extended(block, sides, width):
    for axis, dim in sides:
        count = lax.axis_size(axis)
        forward = [(i, i + 1) for i in range(count - 1)]
        forward.append((count - 1, 0))
        backward = [(target, source) for source, target in forward]
        low = lax.ppermute(
            lax.slice_in_dim(block, block.shape[dim] - width, None, axis=dim), axis, forward
        )
        high = lax.ppermute(lax.slice_in_dim(block, 0, width, axis=dim), axis, backward)
        block = jnp.concatenate([low, block, high], axis=dim)
    return block


def strip_of(block, slot):
    strip_number = slot if slot < 4 else slot - 1
    return block[strip_number * B_SIDE : (strip_number + 1) * B_SIDE]


def mirrored_cells(block):
    empty = jnp.zeros((B_SIDE, block.shape[1]), block.dtype)
    rows_out = []
    for lat_cell in range(3):
        cells = []
        for lon_cell in range(3):
            slot = (2 - lat_cell) * 3 + (2 - lon_cell)
            cells.append(empty if slot == 4 else strip_of(block, slot))
        rows_out.append(jnp.stack(cells))
    return jnp.stack(rows_out)


def local(
    grid_latent,
    mesh_latent,
    edge_geometry,
    senders,
    receivers,
    w_grid,
    w_mesh,
    w_edge,
    edge_bias,
    w_message,
    w_node,
    w_output,
    norm_gain,
    norm_bias,
):
    grid_rows = grid_latent[0, 0]
    own_mesh = mesh_latent[0, 0]
    geometry = edge_geometry[0, 0]
    sources = senders[0, 0]
    targets = receivers[0, 0]
    mesh_rows = own_mesh.shape[0]
    features = own_mesh.shape[1]
    edge_count = sources.shape[0]
    border_total = 8 * B_SIDE
    padded = extended(mirrored_cells(own_mesh), (("lon", 1), ("lat", 0)), 1)
    received = jnp.concatenate([padded[2 * (s // 3), 2 * (s % 3)] for s in border_slots], axis=0)
    mesh_table = jnp.dot(
        jnp.concatenate([own_mesh, received], axis=0), w_mesh, preferred_element_type=jnp.float32
    )
    slot_number = targets // mesh_rows
    row_number = targets % mesh_rows
    table_index = jnp.where(slot_number == 4, row_number, mesh_rows + row_number)
    slot_total = mesh_rows + border_total
    grid_proj = jnp.dot(grid_rows, w_grid, preferred_element_type=jnp.float32)
    edge_block = min(512, edge_count)
    block_count = edge_count // edge_block
    source_blocks = sources.reshape(block_count, edge_block)
    target_blocks = table_index.reshape(block_count, edge_block)
    geometry_blocks = jnp.transpose(geometry.reshape(4, block_count, edge_block), (1, 0, 2))
    slot_ids = jnp.arange(slot_total, dtype=jnp.int32)

    def add_block(summed, items):
        block_sources, block_targets, block_geometry = items
        grid_term = jnp.take(grid_proj, block_sources, axis=0)
        mesh_term = jnp.take(mesh_table, block_targets, axis=0)
        edge_term = jnp.dot(block_geometry.T, w_edge)
        hidden = jax.nn.silu(grid_term + mesh_term + edge_term + edge_bias).astype(jnp.bfloat16)
        message = jnp.dot(hidden, w_message, preferred_element_type=jnp.float32).astype(
            jnp.bfloat16
        )
        target_onehot = (block_targets[:, None] == slot_ids[None, :]).astype(jnp.bfloat16)
        added = lax.dot_general(
            target_onehot, message, (((0,), (0,)), ((), ())), preferred_element_type=jnp.float32
        )
        return (summed + added, None)

    partial_value, _ = lax.scan(
        add_block,
        jnp.zeros((slot_total, features), jnp.float32),
        (source_blocks, target_blocks, geometry_blocks),
    )
    own_part = partial_value[:mesh_rows]
    border_part = partial_value[mesh_rows:]
    empty = jnp.zeros((B_SIDE, features), jnp.float32)
    cells = jnp.stack(
        [
            jnp.stack(
                [empty if a * 3 + b == 4 else strip_of(border_part, a * 3 + b) for b in range(3)]
            )
            for a in range(3)
        ]
    )
    padded = extended(cells.astype(jnp.bfloat16), (("lon", 1), ("lat", 0)), 1).astype(cells.dtype)
    arrived = jnp.concatenate(
        [padded[2 * (2 - s // 3), 2 * (2 - s % 3)] for s in border_slots], axis=0
    )
    arrived = jnp.concatenate(
        [arrived, jnp.zeros((mesh_rows - border_total, features), jnp.float32)], axis=0
    )
    aggregated = own_part + arrived
    node_in = jnp.concatenate([own_mesh, aggregated.astype(jnp.bfloat16)], axis=1)
    node_hidden = jax.nn.silu(jnp.dot(node_in, w_node, preferred_element_type=jnp.float32)).astype(
        jnp.bfloat16
    )
    update = jnp.dot(node_hidden, w_output, preferred_element_type=jnp.float32)
    row_mean = jnp.mean(update, axis=-1, keepdims=True)
    centered = update - row_mean
    row_var = jnp.mean(centered * centered, axis=-1, keepdims=True)
    normed = centered * lax.rsqrt(row_var + 1e-05) * norm_gain + norm_bias
    mesh_out = (own_mesh.astype(jnp.float32) + normed).astype(jnp.bfloat16)
    return mesh_out[None, None]


def solution(mesh):
    return jax.shard_map(
        local,
        mesh=mesh,
        in_specs=(
            P("lat", "lon", None, None),
            P("lat", "lon", None, None),
            P("lat", "lon", None, None),
            P("lat", "lon", None),
            P("lat", "lon", None),
            P(),
            P(),
            P(),
            P(),
            P(),
            P(),
            P(),
            P(),
            P(),
        ),
        out_specs=P("lat", "lon", None, None),
        check_vma=False,
    )
```

profile of v0, /device:TPU:23, one launch (start us, length us, event | category | flops | bytes accessed | tf_op | source)
XLA Modules:
  0.0 81.7 jit_solution(3146070037530898164)
XLA Ops:
  0.0 0.9 %slice_bitcast_fusion.31 = (bf16[1,16,512]{2,1,0:T(8,128)(2,1)S(1)}, bf16[1,16,512]{2,1,0:T(8,128)(2,1)S(1)}, bf16[1,16,512]{2,1,0:T(8,128)(2,1)S(1)}, bf16[1,16...) fusion(bf16[1,1,160,512]{3,2,1,0:T(8,128)(2,1)} %param.17), kind=kLoop, calls=%fused_computation.109 | loop fusion | bytes 262144 | tf_op jit(solution)/shard_map/stack | solution.py:39
  0.9 0.1 pad.38.clone
  1.0 0.1 maximum_bitcast_fusion
  1.1 2.3 %collective-permute-start = (bf16[3,1,16,512]{3,2,1,0:T(8,128)(2,1)S(1)}, bf16[3,1,16,512]{3,2,1,0:T(8,128)(2,1)S(1)}, u32[]{:S(2)}, u32[]{:S(2)}) collective-permute-start(bf16[3,1,16,512]{3,2,1,0:T(8,128)(2,1)S(1)} %get-tuple-element.148), channel_id=1, source_target_pairs={{0,16},{16,32},{32,48},{48,64},{64,80},{80,96},{96,112},{112,128},... | collective-permute-start | bytes 147464 | tf_op jit(solution)/shard_map/ppermute | solution.py:18
  3.4 0.9 %constant_dynamic-update-slice_fusion.8 = bf16[288,512]{1,0:T(8,128)(2,1)S(1)} fusion(bf16[1,1,160,512]{3,2,1,0:T(8,128)(2,1)} %param.17), kind=kLoop, calls=%fused_computation.67 | loop fusion | bytes 327680
  4.4 0.0 copy-start.6
  4.4 0.8 divide_reduce_fusion
  5.2 0.0 copy-start.4
  5.2 0.0 copy-start.11
  5.2 3.1 %fusion.7 = f32[1024,512]{1,0:T(8,128)} fusion(bf16[512,512]{1,0:T(8,128)(2,1)} %param.21, bf16[1,1,1024,512]{3,2,1,0:T(8,128)(2,1)S(1)} %copy-done), kind=kOutput, calls=%fused_computation.23 | convolution fusion | flops 536870912 | bytes 3670016 | tf_op jit(solution)/shard_map/dot_general | solution.py:77
  8.4 2.1 %collective-permute-done.1 = bf16[3,1,16,512]{3,2,1,0:T(8,128)(2,1)S(1)} collective-permute-done((bf16[3,1,16,512]{3,2,1,0:T(8,128)(2,1)S(1)}, bf16[3,1,16,512]{3,2,1,0:T(8,128)(2,1)S(1)}, u32[]{:S(2)}, u32[]{:S(2)}) %collective-permute-start.1) | collective-permute-done | bytes 49184 | tf_op jit(solution)/shard_map/ppermute | solution.py:21
  10.6 0.1 collective-permute-start.2
  10.7 0.5 broadcast.127
  11.3 0.7 reduce.13
  12.0 5.6 %collective-permute-start.3 = (bf16[1,5,16,512]{3,2,1,0:T(8,128)(2,1)S(1)}, bf16[1,5,16,512]{3,2,1,0:T(8,128)(2,1)S(1)}, u32[]{:S(2)}, u32[]{:S(2)}) collective-permute-start(bf16[1,5,16,512]{3,2,1,0:T(8,128)(2,1)S(1)} %get-tuple-element.136), channel_id=1, source_target_pairs={{1,0},{2,1},{3,2},{4,3},{5,4},{6,5},{7,6},{8,7},{9,8},{10,9},{11,1... | collective-permute-start | bytes 245768 | tf_op jit(solution)/shard_map/ppermute | solution.py:21
  17.5 1.1 %collective-permute-done.2 = bf16[1,5,16,512]{3,2,1,0:T(8,128)(2,1)S(1)} collective-permute-done((bf16[1,5,16,512]{3,2,1,0:T(8,128)(2,1)S(1)}, bf16[1,5,16,512]{3,2,1,0:T(8,128)(2,1)S(1)}, u32[]{:S(2)}, u32[]{:S(2)}) %collective-permute-start.2) | collective-permute-done | bytes 81952 | tf_op jit(solution)/shard_map/ppermute | solution.py:18
  18.6 0.4 collective-permute-done.3
  19.0 0.3 fusion.27
  19.4 42.6 %while.11 = (s32[]{:T(128)}, f32[288,512]{1,0:T(8,128)S(1)}, s32[4,512]{1,0:T(4,128)S(1)}, s32[4,512]{1,0:T(4,128)S(1)}, f32[1024,512]{1,0:T(8,128)}, /*index=5*...) while((s32[]{:T(128)}, f32[288,512]{1,0:T(8,128)S(1)}, ...), condition=%wide.region_1.2_spmd.clone, body=%wide.region_0.1_spmd.clone.sunk | while | flops 424864768 | bytes 9091207 | solution.py:100
  19.4 1.6 %gather_fusion = f32[512,512]{1,0:T(8,128)S(1)} fusion(f32[288,512]{1,0:T(8,128)S(1)} %get-tuple-element.252, s32[1024]{0:T(1024)S(1)} %pad_clamp_fusion.4), kind=kCustom, calls=%fused_computation.1.clone.clone.1 | custom fusion | bytes 2099200 | tf_op jit(solution)/shard_map/while/body/eval_jaxpr/jit(_take)/gather | solution.py:88
  21.1 4.3 %gather_fusion.1 = f32[512,512]{1,0:T(8,128)} fusion(f32[1024,512]{1,0:T(8,128)} %get-tuple-element.251, s32[1024]{0:T(1024)S(1)} %pad_clamp_fusion.5), kind=kCustom, calls=%fused_computation.clone.clone.1 | custom fusion | bytes 2099200 | tf_op jit(solution)/shard_map/while/body/eval_jaxpr/jit(_take)/gather | solution.py:87
  25.4 2.6 %multiply_convert_fusion.3 = bf16[512,512]{1,0:T(8,128)(2,1)} fusion(bf16[4,512]{1,0:T(4,128)(2,1)S(1)} %get-tuple-element.254, f32[512,512]{1,0:T(8,128)S(1)} %gather_fusion, f32[512,512]{1,0:T(8,128)} %gather_fusion.1, f32[512]{0:T(512)S(1)} %get-tuple-element.255, pred[512]{0:T(512)(128)(4,1)S(1)} %compare_and_fusion.4, ...), kind=kOutput, calls=%fused_computation.7.clone.1 | convolution fusion | flops 4718592 | bytes 2632708 | tf_op jit(solution)/shard_map/while/body/eval_jaxpr/dot_general | solution.py:89
  28.0 2.0 %convolution_add_fusion.3 = f32[288,512]{1,0:T(8,128)S(1)} fusion(bf16[512,512]{1,0:T(8,128)(2,1)} %multiply_convert_fusion.3, bf16[512,512]{1,0:T(8,128)(2,1)} %get-tuple-element.256, f32[288,512]{1,0:T(8,128)S(1)} %get-tuple-element.236, s32[512]{0:T(512)S(1)} %bitcast.159, pred[]{:T(512)S(6)} %compare.3), kind=kOutput, calls=%fused_computation.6.clone.1 | convolution fusion | flops 420134912 | bytes 2230273 | tf_op jit(solution)/shard_map/while/body/eval_jaxpr/dot_general | solution.py:95
  30.1 1.6 %gather_fusion = f32[512,512]{1,0:T(8,128)S(1)} fusion(f32[288,512]{1,0:T(8,128)S(1)} %get-tuple-element.252, s32[1024]{0:T(1024)S(1)} %pad_clamp_fusion.4), kind=kCustom, calls=%fused_computation.1.clone.clone.1 | custom fusion | bytes 2099200 | tf_op jit(solution)/shard_map/while/body/eval_jaxpr/jit(_take)/gather | solution.py:88
  31.7 4.3 %gather_fusion.1 = f32[512,512]{1,0:T(8,128)} fusion(f32[1024,512]{1,0:T(8,128)} %get-tuple-element.251, s32[1024]{0:T(1024)S(1)} %pad_clamp_fusion.5), kind=kCustom, calls=%fused_computation.clone.clone.1 | custom fusion | bytes 2099200 | tf_op jit(solution)/shard_map/while/body/eval_jaxpr/jit(_take)/gather | solution.py:87
  36.0 2.6 %multiply_convert_fusion.3 = bf16[512,512]{1,0:T(8,128)(2,1)} fusion(bf16[4,512]{1,0:T(4,128)(2,1)S(1)} %get-tuple-element.254, f32[512,512]{1,0:T(8,128)S(1)} %gather_fusion, f32[512,512]{1,0:T(8,128)} %gather_fusion.1, f32[512]{0:T(512)S(1)} %get-tuple-element.255, pred[512]{0:T(512)(128)(4,1)S(1)} %compare_and_fusion.4, ...), kind=kOutput, calls=%fused_computation.7.clone.1 | convolution fusion | flops 4718592 | bytes 2632708 | tf_op jit(solution)/shard_map/while/body/eval_jaxpr/dot_general | solution.py:89
  38.7 2.0 %convolution_add_fusion.3 = f32[288,512]{1,0:T(8,128)S(1)} fusion(bf16[512,512]{1,0:T(8,128)(2,1)} %multiply_convert_fusion.3, bf16[512,512]{1,0:T(8,128)(2,1)} %get-tuple-element.256, f32[288,512]{1,0:T(8,128)S(1)} %get-tuple-element.236, s32[512]{0:T(512)S(1)} %bitcast.159, pred[]{:T(512)S(6)} %compare.3), kind=kOutput, calls=%fused_computation.6.clone.1 | convolution fusion | flops 420134912 | bytes 2230273 | tf_op jit(solution)/shard_map/while/body/eval_jaxpr/dot_general | solution.py:95
  40.7 1.6 %gather_fusion = f32[512,512]{1,0:T(8,128)S(1)} fusion(f32[288,512]{1,0:T(8,128)S(1)} %get-tuple-element.252, s32[1024]{0:T(1024)S(1)} %pad_clamp_fusion.4), kind=kCustom, calls=%fused_computation.1.clone.clone.1 | custom fusion | bytes 2099200 | tf_op jit(solution)/shard_map/while/body/eval_jaxpr/jit(_take)/gather | solution.py:88
  42.3 4.3 %gather_fusion.1 = f32[512,512]{1,0:T(8,128)} fusion(f32[1024,512]{1,0:T(8,128)} %get-tuple-element.251, s32[1024]{0:T(1024)S(1)} %pad_clamp_fusion.5), kind=kCustom, calls=%fused_computation.clone.clone.1 | custom fusion | bytes 2099200 | tf_op jit(solution)/shard_map/while/body/eval_jaxpr/jit(_take)/gather | solution.py:87
  46.7 2.6 %multiply_convert_fusion.3 = bf16[512,512]{1,0:T(8,128)(2,1)} fusion(bf16[4,512]{1,0:T(4,128)(2,1)S(1)} %get-tuple-element.254, f32[512,512]{1,0:T(8,128)S(1)} %gather_fusion, f32[512,512]{1,0:T(8,128)} %gather_fusion.1, f32[512]{0:T(512)S(1)} %get-tuple-element.255, pred[512]{0:T(512)(128)(4,1)S(1)} %compare_and_fusion.4, ...), kind=kOutput, calls=%fused_computation.7.clone.1 | convolution fusion | flops 4718592 | bytes 2632708 | tf_op jit(solution)/shard_map/while/body/eval_jaxpr/dot_general | solution.py:89
  49.3 2.0 %convolution_add_fusion.3 = f32[288,512]{1,0:T(8,128)S(1)} fusion(bf16[512,512]{1,0:T(8,128)(2,1)} %multiply_convert_fusion.3, bf16[512,512]{1,0:T(8,128)(2,1)} %get-tuple-element.256, f32[288,512]{1,0:T(8,128)S(1)} %get-tuple-element.236, s32[512]{0:T(512)S(1)} %bitcast.159, pred[]{:T(512)S(6)} %compare.3), kind=kOutput, calls=%fused_computation.6.clone.1 | convolution fusion | flops 420134912 | bytes 2230273 | tf_op jit(solution)/shard_map/while/body/eval_jaxpr/dot_general | solution.py:95
  51.3 1.6 %gather_fusion = f32[512,512]{1,0:T(8,128)S(1)} fusion(f32[288,512]{1,0:T(8,128)S(1)} %get-tuple-element.252, s32[1024]{0:T(1024)S(1)} %pad_clamp_fusion.4), kind=kCustom, calls=%fused_computation.1.clone.clone.1 | custom fusion | bytes 2099200 | tf_op jit(solution)/shard_map/while/body/eval_jaxpr/jit(_take)/gather | solution.py:88
  53.0 4.3 %gather_fusion.1 = f32[512,512]{1,0:T(8,128)} fusion(f32[1024,512]{1,0:T(8,128)} %get-tuple-element.251, s32[1024]{0:T(1024)S(1)} %pad_clamp_fusion.5), kind=kCustom, calls=%fused_computation.clone.clone.1 | custom fusion | bytes 2099200 | tf_op jit(solution)/shard_map/while/body/eval_jaxpr/jit(_take)/gather | solution.py:87
  57.3 2.6 %multiply_convert_fusion.3 = bf16[512,512]{1,0:T(8,128)(2,1)} fusion(bf16[4,512]{1,0:T(4,128)(2,1)S(1)} %get-tuple-element.254, f32[512,512]{1,0:T(8,128)S(1)} %gather_fusion, f32[512,512]{1,0:T(8,128)} %gather_fusion.1, f32[512]{0:T(512)S(1)} %get-tuple-element.255, pred[512]{0:T(512)(128)(4,1)S(1)} %compare_and_fusion.4, ...), kind=kOutput, calls=%fused_computation.7.clone.1 | convolution fusion | flops 4718592 | bytes 2632708 | tf_op jit(solution)/shard_map/while/body/eval_jaxpr/dot_general | solution.py:89
  60.0 2.0 %convolution_add_fusion.3 = f32[288,512]{1,0:T(8,128)S(1)} fusion(bf16[512,512]{1,0:T(8,128)(2,1)} %multiply_convert_fusion.3, bf16[512,512]{1,0:T(8,128)(2,1)} %get-tuple-element.256, f32[288,512]{1,0:T(8,128)S(1)} %get-tuple-element.236, s32[512]{0:T(512)S(1)} %bitcast.159, pred[]{:T(512)S(6)} %compare.3), kind=kOutput, calls=%fused_computation.6.clone.1 | convolution fusion | flops 420134912 | bytes 2230273 | tf_op jit(solution)/shard_map/while/body/eval_jaxpr/dot_general | solution.py:95
  62.0 0.0 copy-start.1
  62.1 0.1 maximum_bitcast_fusion.4
  62.2 3.6 %collective-permute-start.4 = (bf16[3,1,16,512]{3,2,1,0:T(8,128)(2,1)S(1)}, bf16[3,1,16,512]{3,2,1,0:T(8,128)(2,1)S(1)}, u32[]{:S(2)}, u32[]{:S(2)}) collective-permute-start(bf16[3,1,16,512]{3,2,1,0:T(8,128)(2,1)S(1)} %get-tuple-element.146), channel_id=1, source_target_pairs={{0,16},{16,32},{32,48},{48,64},{64,80},{80,96},{96,112},{112,128},... | collective-permute-start | bytes 147464 | tf_op jit(solution)/shard_map/ppermute | solution.py:18
  65.8 1.2 %collective-permute-done.4 = bf16[3,1,16,512]{3,2,1,0:T(8,128)(2,1)S(1)} collective-permute-done((bf16[3,1,16,512]{3,2,1,0:T(8,128)(2,1)S(1)}, bf16[3,1,16,512]{3,2,1,0:T(8,128)(2,1)S(1)}, u32[]{:S(2)}, u32[]{:S(2)}) %collective-permute-start.4) | collective-permute-done | bytes 49184 | tf_op jit(solution)/shard_map/ppermute | solution.py:18
  66.9 6.0 %collective-permute-done.5 = bf16[3,1,16,512]{3,2,1,0:T(8,128)(2,1)S(1)} collective-permute-done((bf16[3,1,16,512]{3,2,1,0:T(8,128)(2,1)S(1)}, bf16[3,1,16,512]{3,2,1,0:T(8,128)(2,1)S(1)}, u32[]{:S(2)}, u32[]{:S(2)}) %collective-permute-start.5) | collective-permute-done | bytes 49184 | tf_op jit(solution)/shard_map/ppermute | solution.py:21
  72.9 0.1 collective-permute-start.6
  73.0 4.9 %collective-permute-start.7 = (bf16[1,5,16,512]{3,2,1,0:T(8,128)(2,1)S(1)}, bf16[1,5,16,512]{3,2,1,0:T(8,128)(2,1)S(1)}, u32[]{:S(2)}, u32[]{:S(2)}) collective-permute-start(bf16[1,5,16,512]{3,2,1,0:T(8,128)(2,1)S(1)} %get-tuple-element.135), channel_id=1, source_target_pairs={{1,0},{2,1},{3,2},{4,3},{5,4},{6,5},{7,6},{8,7},{9,8},{10,9},{11,1... | collective-permute-start | bytes 245768 | tf_op jit(solution)/shard_map/ppermute | solution.py:21
  77.9 1.7 %collective-permute-done.6 = bf16[1,5,16,512]{3,2,1,0:T(8,128)(2,1)S(1)} collective-permute-done((bf16[1,5,16,512]{3,2,1,0:T(8,128)(2,1)S(1)}, bf16[1,5,16,512]{3,2,1,0:T(8,128)(2,1)S(1)}, u32[]{:S(2)}, u32[]{:S(2)}) %collective-permute-start.6) | collective-permute-done | bytes 81952 | tf_op jit(solution)/shard_map/ppermute | solution.py:18
  79.6 0.1 maximum_convert_fusion
  79.8 0.1 add_convert_fusion.1
  79.9 0.7 fusion.24
  80.6 0.2 multiply_reduce_fusion
  80.9 0.8 %fusion.18 = bf16[1,1,160,512]{3,2,1,0:T(8,128)(2,1)} fusion(f32[160,512]{1,0:T(8,128)S(1)} %get-tuple-element.151, f32[512]{0:T(512)S(1)} %copy-done.7, f32[512]{0:T(512)S(1)} %copy-done.8, f32[160]{0:T(256)S(1)} %add_rsqrt_fusion, f32[160]{0:T(256)S(1)} %broadcast_multiply_fusion, bf16[1,1,160,512]{3,2,1,0:T(8,128)(2,1)S(1)} %copy-done.1), kind=kLoop, calls=%fused_computation.35 | loop fusion | flops 573440 | bytes 660736 | tf_op jit(solution)/shard_map/broadcast_in_dim | solution.py:134
  (81 shorter events, 0.6 us)
Async XLA Ops:
  0.0 5.2 %copy-start = (bf16[1,1,1024,512]{3,2,1,0:T(8,128)(2,1)S(1)}, bf16[1,1,1024,512]{3,2,1,0:T(8,128)(2,1)}, u32[]{:S(2)}) copy-start(bf16[1,1,1024,512]{3,2,1,0:T(8,128)(2,1)} %param.16) | copy-start | bytes 3145732
  1.1 7.2 %copy-start.3 = (s32[1,1,2048]{2,1,0:T(1,128)S(1)}, s32[1,1,2048]{2,1,0:T(1,128)}, u32[]{:S(2)}) copy-start(s32[1,1,2048]{2,1,0:T(1,128)} %param.20) | copy-start | bytes 24580
  1.1 7.3 %collective-permute-start = (bf16[3,1,16,512]{3,2,1,0:T(8,128)(2,1)S(1)}, bf16[3,1,16,512]{3,2,1,0:T(8,128)(2,1)S(1)}, u32[]{:S(2)}, u32[]{:S(2)}) collective-permute-start(bf16[3,1,16,512]{3,2,1,0:T(8,128)(2,1)S(1)} %get-tuple-element.148), channel_id=1, source_target_pairs={{0,16},{16,32},{32,48},{48,64},{64,80},{80,96},{96,112},{112,128},... | collective-permute-start | bytes 147464 | tf_op jit(solution)/shard_map/ppermute | solution.py:18
  3.4 7.1 %collective-permute-start.1 = (bf16[3,1,16,512]{3,2,1,0:T(8,128)(2,1)S(1)}, bf16[3,1,16,512]{3,2,1,0:T(8,128)(2,1)S(1)}, u32[]{:S(2)}, u32[]{:S(2)}) collective-permute-start(bf16[3,1,16,512]{3,2,1,0:T(8,128)(2,1)S(1)} %get-tuple-element.149), channel_id=1, source_target_pairs={{16,0},{32,16},{48,32},{64,48},{80,64},{96,80},{112,96},{128,112},... | collective-permute-start | bytes 147464 | tf_op jit(solution)/shard_map/ppermute | solution.py:21
  4.4 6.9 %copy-start.6 = (s32[1,1,2048]{2,1,0:T(1,128)S(1)}, s32[1,1,2048]{2,1,0:T(1,128)}, u32[]{:S(2)}) copy-start(s32[1,1,2048]{2,1,0:T(1,128)} %param.19) | copy-start | bytes 24580
  5.2 6.8 %copy-start.4 = (f32[1,1,4,2048]{3,2,1,0:T(4,128)S(1)}, f32[1,1,4,2048]{3,2,1,0:T(4,128)}, u32[]{:S(2)}) copy-start(f32[1,1,4,2048]{3,2,1,0:T(4,128)} %param.18) | copy-start | bytes 98308
  5.2 6.8 %copy-start.5 = (f32[4,512]{1,0:T(4,128)S(1)}, f32[4,512]{1,0:T(4,128)}, u32[]{:S(2)}) copy-start(f32[4,512]{1,0:T(4,128)} %param.23) | copy-start | bytes 24580
  5.2 13.9 %copy-start.2 = (bf16[512,512]{1,0:T(8,128)(2,1)S(1)}, bf16[512,512]{1,0:T(8,128)(2,1)}, u32[]{:S(2)}) copy-start(bf16[512,512]{1,0:T(8,128)(2,1)} %param.22) | copy-start | bytes 1572868
  5.2 14.2 %copy-start.11 = (f32[512]{0:T(512)S(1)}, f32[512]{0:T(512)}, u32[]{:S(2)}) copy-start(f32[512]{0:T(512)} %param.24) | copy-start | bytes 6148
  10.6 8.0 %collective-permute-start.2 = (bf16[1,5,16,512]{3,2,1,0:T(8,128)(2,1)S(1)}, bf16[1,5,16,512]{3,2,1,0:T(8,128)(2,1)S(1)}, u32[]{:S(2)}, u32[]{:S(2)}) collective-permute-start(bf16[1,5,16,512]{3,2,1,0:T(8,128)(2,1)S(1)} %get-tuple-element.137), channel_id=1, source_target_pairs={{0,1},{1,2},{2,3},{3,4},{4,5},{5,6},{6,7},{7,8},{8,9},{9,10},{10,1... | collective-permute-start | bytes 245768 | tf_op jit(solution)/shard_map/ppermute | solution.py:18
  12.0 7.0 %collective-permute-start.3 = (bf16[1,5,16,512]{3,2,1,0:T(8,128)(2,1)S(1)}, bf16[1,5,16,512]{3,2,1,0:T(8,128)(2,1)S(1)}, u32[]{:S(2)}, u32[]{:S(2)}) collective-permute-start(bf16[1,5,16,512]{3,2,1,0:T(8,128)(2,1)S(1)} %get-tuple-element.136), channel_id=1, source_target_pairs={{1,0},{2,1},{3,2},{4,3},{5,4},{6,5},{7,6},{8,7},{9,8},{10,9},{11,1... | collective-permute-start | bytes 245768 | tf_op jit(solution)/shard_map/ppermute | solution.py:21
  62.0 17.9 %copy-start.1 = (bf16[1,1,160,512]{3,2,1,0:T(8,128)(2,1)S(1)}, bf16[1,1,160,512]{3,2,1,0:T(8,128)(2,1)}, u32[]{:S(2)}) copy-start(bf16[1,1,160,512]{3,2,1,0:T(8,128)(2,1)} %param.17) | copy-start | bytes 491524
  62.0 17.9 %copy-start.9 = (bf16[1024,512]{1,0:T(8,128)(2,1)S(1)}, bf16[1024,512]{1,0:T(8,128)(2,1)}, u32[]{:S(2)}) copy-start(bf16[1024,512]{1,0:T(8,128)(2,1)} %param.26) | copy-start | bytes 3145732
  62.0 17.9 %copy-start.10 = (bf16[512,512]{1,0:T(8,128)(2,1)S(1)}, bf16[512,512]{1,0:T(8,128)(2,1)}, u32[]{:S(2)}) copy-start(bf16[512,512]{1,0:T(8,128)(2,1)} %param.27) | copy-start | bytes 1572868
  62.2 4.7 %collective-permute-start.4 = (bf16[3,1,16,512]{3,2,1,0:T(8,128)(2,1)S(1)}, bf16[3,1,16,512]{3,2,1,0:T(8,128)(2,1)S(1)}, u32[]{:S(2)}, u32[]{:S(2)}) collective-permute-start(bf16[3,1,16,512]{3,2,1,0:T(8,128)(2,1)S(1)} %get-tuple-element.146), channel_id=1, source_target_pairs={{0,16},{16,32},{32,48},{48,64},{64,80},{80,96},{96,112},{112,128},... | collective-permute-start | bytes 147464 | tf_op jit(solution)/shard_map/ppermute | solution.py:18
  65.7 7.1 %collective-permute-start.5 = (bf16[3,1,16,512]{3,2,1,0:T(8,128)(2,1)S(1)}, bf16[3,1,16,512]{3,2,1,0:T(8,128)(2,1)S(1)}, u32[]{:S(2)}, u32[]{:S(2)}) collective-permute-start(bf16[3,1,16,512]{3,2,1,0:T(8,128)(2,1)S(1)} %get-tuple-element.147), channel_id=1, source_target_pairs={{16,0},{32,16},{48,32},{64,48},{80,64},{96,80},{112,96},{128,112},... | collective-permute-start | bytes 147464 | tf_op jit(solution)/shard_map/ppermute | solution.py:21
  72.9 6.7 %collective-permute-start.6 = (bf16[1,5,16,512]{3,2,1,0:T(8,128)(2,1)S(1)}, bf16[1,5,16,512]{3,2,1,0:T(8,128)(2,1)S(1)}, u32[]{:S(2)}, u32[]{:S(2)}) collective-permute-start(bf16[1,5,16,512]{3,2,1,0:T(8,128)(2,1)S(1)} %get-tuple-element.134), channel_id=1, source_target_pairs={{0,1},{1,2},{2,3},{3,4},{4,5},{5,6},{6,7},{7,8},{8,9},{9,10},{10,1... | collective-permute-start | bytes 245768 | tf_op jit(solution)/shard_map/ppermute | solution.py:18
  73.0 6.6 %collective-permute-start.7 = (bf16[1,5,16,512]{3,2,1,0:T(8,128)(2,1)S(1)}, bf16[1,5,16,512]{3,2,1,0:T(8,128)(2,1)S(1)}, u32[]{:S(2)}, u32[]{:S(2)}) collective-permute-start(bf16[1,5,16,512]{3,2,1,0:T(8,128)(2,1)S(1)} %get-tuple-element.135), channel_id=1, source_target_pairs={{1,0},{2,1},{3,2},{4,3},{5,4},{6,5},{7,6},{8,7},{9,8},{10,9},{11,1... | collective-permute-start | bytes 245768 | tf_op jit(solution)/shard_map/ppermute | solution.py:21
  79.9 1.0 %copy-start.7 = (f32[512]{0:T(512)S(1)}, f32[512]{0:T(512)}, u32[]{:S(2)}) copy-start(f32[512]{0:T(512)} %param.29) | copy-start | bytes 6148
  79.9 1.0 %copy-start.8 = (f32[512]{0:T(512)S(1)}, f32[512]{0:T(512)}, u32[]{:S(2)}) copy-start(f32[512]{0:T(512)} %param.28) | copy-start | bytes 6148
where the time goes:
time: 82.3 us; the launch traced here: 81.7 us
  local copies, waits for them, and re-layouts  26.5 us (32%)
  matrix products  22.5 us (27%)
  starting transfers between devices  16.5 us (20%)
  waiting for transfers between devices  12.5 us (15%)
  other arithmetic  3.14 us (4%)
    gather x4, local copies, waits for them, and re-layouts, add_block(): grid_term = jnp.take(grid_proj, block_sources, axis=0)  17.3 us
    dot_general x4, matrix products, add_block(): edge_term = jnp.dot(block_geometry.T, w_edge)  10.5 us
    ppermute x4, starting transfers between devices, extended(): lax.ppermute(lax.slice_in_dim(block, 0, width, axis=dim), axis, backward)  10.4 us
    ppermute x4, waiting for transfers between devices, extended(): lax.ppermute(lax.slice_in_dim(block, 0, width, axis=dim), axis, backward)  8.48 us
    dot_general x4, matrix products, add_block(): lax.dot_general(target_onehot, message, (((0,), (0,)), ((), ())), preferr...  7.89 us
    gather x4, local copies, waits for them, and re-layouts, add_block(): mesh_term = jnp.take(mesh_table, block_targets, axis=0)  6.48 us
    ppermute x4, starting transfers between devices, extended(): lax.ppermute(lax.slice_in_dim(block, block.shape[dim] - width, None, axis...  6.05 us
    ppermute x4, waiting for transfers between devices, extended(): lax.ppermute(lax.slice_in_dim(block, block.shape[dim] - width, None, axis...  3.98 us
  transfers between devices with their start and end apart: 8, of which 6 were waited for; matrix products, arithmetic and copies ran while one was open for 8% of the time, Pallas kernels for 0%

commit v1 on v0

v1 whole, which is shorter than its diff:
```python
import functools

import jax
import jax.numpy as jnp
from jax import lax
from jax.experimental import pallas as pl
from jax.experimental.pallas import tpu as pltpu
from jax.sharding import PartitionSpec as P

B_SIDE = 16
BORDER = 8 * B_SIDE
EXTRA_AT = 160
BLOCK = 512
F32 = jnp.float32
BF16 = jnp.bfloat16
SLOTS = (0, 1, 2, 3, 5, 6, 7, 8)


def onehot(codes, picks):
    return jnp.where(codes == picks, jnp.ones((), BF16), jnp.zeros((), BF16))


def silu(x):
    half = 0.5 * x
    return half + half * jnp.tanh(half)


def dot(a, b):
    return jnp.dot(a, b, preferred_element_type=F32)


def dot_nt(a, b):
    return lax.dot_general(a, b, (((1,), (1,)), ((), ())), preferred_element_type=F32)


def pieces(x):
    first = x.astype(BF16).astype(F32)
    rest = x - first
    second = rest.astype(BF16).astype(F32)
    return first, second, rest - second


def kernel(
    n_lat,
    n_lon,
    grid_h,
    mesh_h,
    geo_h,
    snd_h,
    rcv_h,
    wg_h,
    wm_h,
    we_h,
    eb_h,
    wmsg_h,
    wnode_h,
    wout_h,
    gain_h,
    nb_h,
    out_ref,
    grid_v,
    mesh_v,
    geo_v,
    snd_v,
    rcv_v,
    wg_v,
    wm_v,
    we_v,
    eb_v,
    wmsg_v,
    wnode_v,
    wout_v,
    gain_v,
    nb_v,
    table_v,
    extra_v,
    gx_v,
    own_v,
    border_v,
    pre_v,
    hid_v,
    near_v,
    part_v,
    arrived_v,
    load_sem,
    send1,
    recv1,
    send2,
    recv2,
):
    lon = lax.axis_index("lon")
    lat = lax.axis_index("lat")
    rows = mesh_v.shape[0]
    features = mesh_v.shape[1]
    grid_rows = grid_v.shape[0]
    edges = snd_v.shape[1]

    def peer(slot, sign):
        up, right = slot // 3 - 1, slot % 3 - 1
        return {
            "lat": lax.rem(lat + sign * up + n_lat, n_lat),
            "lon": lax.rem(lon + sign * right + n_lon, n_lon),
        }

    barrier = pltpu.get_barrier_semaphore()
    for slot in SLOTS:
        pl.semaphore_signal(
            barrier, inc=1, device_id=peer(slot, 1), device_id_type=pl.DeviceIdType.MESH
        )
    loads = {}
    order = (
        ("mesh", mesh_h, mesh_v),
        ("wm", wm_h, wm_v),
        ("we", we_h, we_v),
        ("eb", eb_h, eb_v),
        ("geo", geo_h, geo_v),
        ("snd", snd_h, snd_v),
        ("rcv", rcv_h, rcv_v),
        ("wg", wg_h, wg_v),
        ("grid", grid_h, grid_v),
        ("wnode", wnode_h, wnode_v),
        ("wmsg", wmsg_h, wmsg_v),
        ("wout", wout_h, wout_v),
        ("gain", gain_h, gain_v),
        ("nb", nb_h, nb_v),
    )
    for number, (name, source, target) in enumerate(order):
        loads[name] = pltpu.make_async_copy(source, target, load_sem.at[number])
        loads[name].start()

    extra_v[...] = jnp.zeros_like(extra_v)
    gx_v[...] = jnp.zeros_like(gx_v)
    for name in ("mesh", "wm", "we", "eb", "geo", "snd", "rcv"):
        loads[name].wait()

    pl.semaphore_wait(barrier, len(SLOTS))
    first = []
    for k, slot in enumerate(SLOTS):
        part = pl.ds(k * B_SIDE, B_SIDE)
        copy = pltpu.make_async_remote_copy(
            src_ref=mesh_v.at[part],
            dst_ref=near_v.at[part],
            send_sem=send1.at[k],
            recv_sem=recv1.at[k],
            device_id=peer(slot, -1),
            device_id_type=pl.DeviceIdType.MESH,
        )
        copy.start()
        first.append(copy)

    w1, w2, w3 = pieces(we_v[...])
    g1, g2, g3 = pieces(geo_v[...])
    base = EXTRA_AT - 128
    for i, (g, w) in enumerate(((g1, w1), (g1, w2), (g2, w1), (g2, w2), (g1, w3), (g3, w1))):
        gx_v[4 * i : 4 * i + 4, :] = g
        extra_v[base + 4 * i : base + 4 * i + 4, :] = w
    gx_v[24:27, :] = jnp.ones((3, edges), F32)
    for i, b in enumerate(pieces(eb_v[...])):
        extra_v[base + 24 + i : base + 25 + i, :] = b

    wm_t = wm_v[...].T
    own_t = dot_nt(wm_t, mesh_v[...])
    own_t = jnp.concatenate(
        [own_t, jnp.zeros((features, 256 - rows), F32)], axis=1
    )
    own_t = own_t + jnp.concatenate([jnp.zeros((features, 128), F32), extra_v[...].T], axis=1)
    table_v[:, grid_rows : grid_rows + 256] = own_t.astype(BF16)

    loads["wg"].wait()
    loads["grid"].wait()
    wg_t = wg_v[...].T
    for at in range(0, grid_rows, 256):
        table_v[:, at : at + 256] = dot_nt(wg_t, grid_v[at : at + 256, :]).astype(BF16)

    i16 = jnp.int16
    grid_codes = lax.broadcasted_iota(jnp.int32, (grid_rows, BLOCK), 0).astype(i16)
    own_codes = (lax.broadcasted_iota(jnp.int32, (rows, BLOCK), 0) + 4 * rows).astype(i16)
    q = lax.broadcasted_iota(jnp.int32, (BORDER, BLOCK), 0)
    border_codes = (q + rows * ((q >> 4) + (q >= 64).astype(jnp.int32))).astype(i16)
    for at in range(0, edges, BLOCK):
        here = pl.ds(at, BLOCK)
        snd = snd_v[:, here].astype(i16)
        rcv = rcv_v[:, here].astype(i16)
        own = onehot(own_codes, rcv)
        own_v[:, here] = own
        border_v[:, here] = onehot(border_codes, rcv)
        stacked = jnp.concatenate(
            [
                onehot(grid_codes, snd),
                own,
                gx_v[:, here].astype(BF16),
                jnp.zeros((256 - rows - 32, BLOCK), BF16),
            ],
            axis=0,
        )
        pre_v[:, here] = dot(table_v[...], stacked)

    for copy in first:
        copy.wait_recv()
    near_t = dot_nt(wm_t, near_v[...]).astype(BF16)
    for at in range(0, edges, BLOCK):
        here = pl.ds(at, BLOCK)
        full = pre_v[:, here] + dot(near_t, border_v[:, here])
        hid_v[:, here] = silu(full).astype(BF16)
    part_v[...] = dot_nt(border_v[...], hid_v[...]).astype(BF16)

    second = []
    for k, slot in enumerate(SLOTS):
        part = pl.ds(k * B_SIDE, B_SIDE)
        copy = pltpu.make_async_remote_copy(
            src_ref=part_v.at[part],
            dst_ref=arrived_v.at[part],
            send_sem=send2.at[k],
            recv_sem=recv2.at[k],
            device_id=peer(slot, 1),
            device_id_type=pl.DeviceIdType.MESH,
        )
        copy.start()
        second.append(copy)

    own_sum = dot_nt(own_v[...], hid_v[...])
    for name in ("wnode", "wmsg", "wout", "gain", "nb"):
        loads[name].wait()
    node_pre = dot(mesh_v[...], wnode_v[0:features, :])
    for copy in first:
        copy.wait_send()
    for copy in second:
        copy.wait_recv()
    total = jnp.concatenate(
        [own_sum[:BORDER] + arrived_v[...].astype(F32), own_sum[BORDER:]], axis=0
    )
    high = total.astype(BF16)
    low = (total - high.astype(F32)).astype(BF16)
    summed = dot(high, wmsg_v[...]) + dot(low, wmsg_v[...])
    node_pre = node_pre + dot(summed.astype(BF16), wnode_v[features : 2 * features, :])
    update = dot(silu(node_pre).astype(BF16), wout_v[...])
    mean = jnp.mean(update, axis=-1, keepdims=True)
    centered = update - mean
    var = jnp.mean(centered * centered, axis=-1, keepdims=True)
    normed = centered * lax.rsqrt(var + 1e-05) * gain_v[...] + nb_v[...]
    out_ref[...] = (mesh_v[...].astype(F32) + normed).astype(BF16)
    for copy in second:
        copy.wait_send()


def solution(mesh):
    n_lat, n_lon = mesh.shape["lat"], mesh.shape["lon"]

    def local(
        grid_latent,
        mesh_latent,
        edge_geometry,
        senders,
        receivers,
        w_grid,
        w_mesh,
        w_edge,
        edge_bias,
        w_message,
        w_node,
        w_output,
        norm_gain,
        norm_bias,
    ):
        args = (
            grid_latent[0, 0],
            mesh_latent[0, 0],
            edge_geometry[0, 0],
            senders[0],
            receivers[0],
            w_grid,
            w_mesh,
            w_edge,
            edge_bias[None],
            w_message,
            w_node,
            w_output,
            norm_gain[None],
            norm_bias[None],
        )
        rows, features = args[1].shape
        edges = senders.shape[2]
        grid_rows = args[0].shape[0]
        out = pl.pallas_call(
            functools.partial(kernel, n_lat, n_lon),
            out_shape=jax.ShapeDtypeStruct((rows, features), BF16),
            in_specs=[pl.BlockSpec(memory_space=pl.ANY)] * len(args),
            out_specs=pl.BlockSpec(memory_space=pltpu.VMEM),
            scratch_shapes=[pltpu.VMEM(a.shape, a.dtype) for a in args]
            + [
                pltpu.VMEM((features, grid_rows + 256), BF16),
                pltpu.VMEM((128, features), F32),
                pltpu.VMEM((32, edges), F32),
                pltpu.VMEM((rows, edges), BF16),
                pltpu.VMEM((BORDER, edges), BF16),
                pltpu.VMEM((features, edges), F32),
                pltpu.VMEM((features, edges), BF16),
                pltpu.VMEM((BORDER, features), BF16),
                pltpu.VMEM((BORDER, features), BF16),
                pltpu.VMEM((BORDER, features), BF16),
                pltpu.SemaphoreType.DMA((len(args),)),
                pltpu.SemaphoreType.DMA((len(SLOTS),)),
                pltpu.SemaphoreType.DMA((len(SLOTS),)),
                pltpu.SemaphoreType.DMA((len(SLOTS),)),
                pltpu.SemaphoreType.DMA((len(SLOTS),)),
            ],
            compiler_params=pltpu.CompilerParams(
                collective_id=0, has_side_effects=True, vmem_limit_bytes=60 * 1024 * 1024
            ),
        )(*args)
        return out[None, None]

    return jax.shard_map(
        local,
        mesh=mesh,
        in_specs=(
            P("lat", "lon", None, None),
            P("lat", "lon", None, None),
            P("lat", "lon", None, None),
            P("lat", "lon", None),
            P("lat", "lon", None),
        )
        + (P(),) * 9,
        out_specs=P("lat", "lon", None, None),
        check_vma=False,
    )
```

time: 82.3 us -> 25.1 us (0.30)
  the two profiles are of different devices: /device:TPU:23 before, /device:TPU:1 now
where the time goes in v1:
time: 25.1 us; the launch traced here: 25 us
  Pallas kernels  23.4 us (93%)
  local copies, waits for them, and re-layouts  1.59 us (6%)
    pallas_call x1, Pallas kernels, local(): pl.pallas_call(functools.partial(kernel, n_lat, n_lon), out_shape=jax.Sha...  23.4 us
    unnamed x1, local copies, waits for them, and re-layouts  1.59 us

profile of v1, /device:TPU:1, one launch (start us, length us, event | category | flops | bytes accessed | tf_op | source)
XLA Modules:
  0.0 25.0 jit_solution(14910910741701383205)
XLA Ops:
  0.0 23.4 %shard_map.136 = bf16[160,512]{1,0:T(8,128)(2,1)} custom-call(bf16[1024,512]{1,0:T(8,128)(2,1)} %bitcast.9, bf16[160,512]{1,0:T(8,128)(2,1)} %bitcast.11, f32[4,2048]{1,0:T(4,128)} %bitcast.12, s32[1,2048]{1,0:T(1,128)} %bitcast.13, s32[1,2048]{1,0:T(1,128)} %bitcast.14, bf16[512,512]{1,0:T(8,128)(2,1)} %wg_h.1, bf16[512,512]{1,0:T(8,128)(2,1)} %wm_h.1, ...), custom_call_target="tpu_custom_call" | custom-call | tf_op jit(solution)/shard_map/pallas_call | solution.py:284
  23.5 1.6 %copy.16 = bf16[1,1,160,512]{3,2,1,0:T(8,128)(2,1)} copy(bf16[1,1,160,512]{3,2,1,0:T(8,128)(2,1)} %bitcast.10) | data formatting | bytes 327680

commit v2 on v1

--- a/solution.py
+++ b/solution.py
@@ -9,11 +9,12 @@
 
 B_SIDE = 16
 BORDER = 8 * B_SIDE
-EXTRA_AT = 160
 BLOCK = 512
+TAIL_BLOCK = 256
 F32 = jnp.float32
 BF16 = jnp.bfloat16
-SLOTS = (0, 1, 2, 3, 5, 6, 7, 8)
+SLOTS = (3, 5, 0, 2, 6, 8, 1, 7)
+CORNER_ROWS = 8
 
 
 def onehot(codes, picks):
@@ -79,6 +80,7 @@
     border_v,
     pre_v,
     hid_v,
+    proj_v,
     near_v,
     part_v,
     arrived_v,
@@ -94,18 +96,48 @@
     features = mesh_v.shape[1]
     grid_rows = grid_v.shape[0]
     edges = snd_v.shape[1]
+    mesh_ids = pl.DeviceIdType.MESH
 
     def peer(slot, sign):
-        up, right = slot // 3 - 1, slot % 3 - 1
-        return {
-            "lat": lax.rem(lat + sign * up + n_lat, n_lat),
-            "lon": lax.rem(lon + sign * right + n_lon, n_lon),
-        }
-
+        up, right = sign * (slot // 3 - 1), sign * (slot % 3 - 1)
+        return {"lat": lat + up, "lon": lax.rem(lon + right + n_lon, n_lon)}
+
+    def if_peer(slot, sign, action):
+        up = sign * (slot // 3 - 1)
+        if up == 0:
+            action()
+        elif up < 0:
+            pl.when(lat > 0)(action)
+        else:
+            pl.when(lat < n_lat - 1)(action)
+
+    def exchange(source, target, send_sem, recv_sem, sign):
+        copies = []
+        for slot in SLOTS:
+            k = slot if slot < 4 else slot - 1
+            part = pl.ds(k * B_SIDE, CORNER_ROWS if slot % 2 == 0 else B_SIDE)
+            copies.append(
+                pltpu.make_async_remote_copy(
+                    src_ref=source.at[part],
+                    dst_ref=target.at[part],
+                    send_sem=send_sem.at[k],
+                    recv_sem=recv_sem.at[k],
+                    device_id=peer(slot, sign),
+                    device_id_type=mesh_ids,
+                )
+            )
+        return copies
+
+    near_v[...] = jnp.zeros_like(near_v)
+    arrived_v[...] = jnp.zeros_like(arrived_v)
     barrier = pltpu.get_barrier_semaphore()
     for slot in SLOTS:
-        pl.semaphore_signal(
-            barrier, inc=1, device_id=peer(slot, 1), device_id_type=pl.DeviceIdType.MESH
+        if_peer(
+            slot,
+            1,
+            lambda: pl.semaphore_signal(
+                barrier, inc=1, device_id=peer(slot, 1), device_id_type=mesh_ids
+            ),
         )
     loads = {}
     order = (
@@ -127,51 +159,37 @@
     for number, (name, source, target) in enumerate(order):
         loads[name] = pltpu.make_async_copy(source, target, load_sem.at[number])
         loads[name].start()
-
     extra_v[...] = jnp.zeros_like(extra_v)
     gx_v[...] = jnp.zeros_like(gx_v)
-    for name in ("mesh", "wm", "we", "eb", "geo", "snd", "rcv"):
+    for name in ("mesh", "wm"):
         loads[name].wait()
-
-    pl.semaphore_wait(barrier, len(SLOTS))
-    first = []
-    for k, slot in enumerate(SLOTS):
-        part = pl.ds(k * B_SIDE, B_SIDE)
-        copy = pltpu.make_async_remote_copy(
-            src_ref=mesh_v.at[part],
-            dst_ref=near_v.at[part],
-            send_sem=send1.at[k],
-            recv_sem=recv1.at[k],
-            device_id=peer(slot, -1),
-            device_id_type=pl.DeviceIdType.MESH,
-        )
-        copy.start()
-        first.append(copy)
+    proj_v[...] = dot(mesh_v[0:BORDER, :], wm_v[...]).astype(BF16)
+    own_t = dot_nt(wm_v[...].T, mesh_v[...])
+    for name in ("we", "eb", "geo", "snd", "rcv"):
+        loads[name].wait()
 
     w1, w2, w3 = pieces(we_v[...])
     g1, g2, g3 = pieces(geo_v[...])
-    base = EXTRA_AT - 128
+    base = rows - 128
     for i, (g, w) in enumerate(((g1, w1), (g1, w2), (g2, w1), (g2, w2), (g1, w3), (g3, w1))):
         gx_v[4 * i : 4 * i + 4, :] = g
         extra_v[base + 4 * i : base + 4 * i + 4, :] = w
     gx_v[24:27, :] = jnp.ones((3, edges), F32)
     for i, b in enumerate(pieces(eb_v[...])):
         extra_v[base + 24 + i : base + 25 + i, :] = b
-
-    wm_t = wm_v[...].T
-    own_t = dot_nt(wm_t, mesh_v[...])
-    own_t = jnp.concatenate(
-        [own_t, jnp.zeros((features, 256 - rows), F32)], axis=1
-    )
+    own_t = jnp.concatenate([own_t, jnp.zeros((features, 256 - rows), F32)], axis=1)
     own_t = own_t + jnp.concatenate([jnp.zeros((features, 128), F32), extra_v[...].T], axis=1)
     table_v[:, grid_rows : grid_rows + 256] = own_t.astype(BF16)
-
+    ends = jnp.where(jnp.logical_or(lat == 0, lat == n_lat - 1), 3, 0)
+    pl.semaphore_wait(barrier, len(SLOTS) - ends)
+    first = exchange(proj_v, near_v, send1, recv1, -1)
+    for slot, copy in zip(SLOTS, first):
+        if_peer(slot, -1, copy.start)
     loads["wg"].wait()
     loads["grid"].wait()
     wg_t = wg_v[...].T
     for at in range(0, grid_rows, 256):
         table_v[:, at : at + 256] = dot_nt(wg_t, grid_v[at : at + 256, :]).astype(BF16)
-
     i16 = jnp.int16
     grid_codes = lax.broadcasted_iota(jnp.int32, (grid_rows, BLOCK), 0).astype(i16)
     own_codes = (lax.broadcasted_iota(jnp.int32, (rows, BLOCK), 0) + 4 * rows).astype(i16)
@@ -194,53 +212,44 @@
             axis=0,
         )
         pre_v[:, here] = dot(table_v[...], stacked)
-
-    for copy in first:
-        copy.wait_recv()
-    near_t = dot_nt(wm_t, near_v[...]).astype(BF16)
-    for at in range(0, edges, BLOCK):
-        here = pl.ds(at, BLOCK)
-        full = pre_v[:, here] + dot(near_t, border_v[:, here])
-        hid_v[:, here] = silu(full).astype(BF16)
-    part_v[...] = dot_nt(border_v[...], hid_v[...]).astype(BF16)
-
-    second = []
-    for k, slot in enumerate(SLOTS):
-        part = pl.ds(k * B_SIDE, B_SIDE)
-        copy = pltpu.make_async_remote_copy(
-            src_ref=part_v.at[part],
-            dst_ref=arrived_v.at[part],
-            send_sem=send2.at[k],
-            recv_sem=recv2.at[k],
-            device_id=peer(slot, 1),
-            device_id_type=pl.DeviceIdType.MESH,
-        )
-        copy.start()
-        second.append(copy)
-
+    for slot, copy in zip(SLOTS, first):
+        if_peer(slot, 1, copy.wait_recv)
+    near_t = near_v[...].T
+    part_sum = jnp.zeros((BORDER, features), F32)
+    ahead = dot(near_t, border_v[:, 0:TAIL_BLOCK])
+    for at in range(0, edges, TAIL_BLOCK):
+        here = pl.ds(at, TAIL_BLOCK)
+        full = pre_v[:, here] + ahead
+        if at + TAIL_BLOCK < edges:
+            ahead = dot(near_t, border_v[:, at + TAIL_BLOCK : at + 2 * TAIL_BLOCK])
+        hidden = silu(full).astype(BF16)
+        hid_v[:, here] = hidden
+        part_sum = part_sum + dot_nt(border_v[:, here], hidden)
+    part_v[...] = part_sum.astype(BF16)
+    second = exchange(part_v, arrived_v, send2, recv2, 1)
+    for slot, copy in zip(SLOTS, second):
+        if_peer(slot, 1, copy.start)
     own_sum = dot_nt(own_v[...], hid_v[...])
     for name in ("wnode", "wmsg", "wout", "gain", "nb"):
         loads[name].wait()
+    joined = dot(wmsg_v[...], wnode_v[features : 2 * features, :]).astype(BF16)
     node_pre = dot(mesh_v[...], wnode_v[0:features, :])
-    for copy in first:
-        copy.wait_send()
-    for copy in second:
-        copy.wait_recv()
+    for slot, copy in zip(SLOTS, first):
+        if_peer(slot, -1, copy.wait_send)
+    for slot, copy in zip(SLOTS, second):
+        if_peer(slot, -1, copy.wait_recv)
     total = jnp.concatenate(
         [own_sum[:BORDER] + arrived_v[...].astype(F32), own_sum[BORDER:]], axis=0
     )
-    high = total.astype(BF16)
-    low = (total - high.astype(F32)).astype(BF16)
-    summed = dot(high, wmsg_v[...]) + dot(low, wmsg_v[...])
-    node_pre = node_pre + dot(summed.astype(BF16), wnode_v[features : 2 * features, :])
+    node_pre = node_pre + dot(total.astype(BF16), joined)
     update = dot(silu(node_pre).astype(BF16), wout_v[...])
     mean = jnp.mean(update, axis=-1, keepdims=True)
     centered = update - mean
     var = jnp.mean(centered * centered, axis=-1, keepdims=True)
     normed = centered * lax.rsqrt(var + 1e-05) * gain_v[...] + nb_v[...]
     out_ref[...] = (mesh_v[...].astype(F32) + normed).astype(BF16)
-    for copy in second:
-        copy.wait_send()
+    for slot, copy in zip(SLOTS, second):
+        if_peer(slot, 1, copy.wait_send)
 
 
 def solution(mesh):
@@ -283,7 +292,7 @@
         grid_rows = args[0].shape[0]
         out = pl.pallas_call(
             functools.partial(kernel, n_lat, n_lon),
-            out_shape=jax.ShapeDtypeStruct((rows, features), BF16),
+            out_shape=pltpu.VMEM((rows, features), BF16),
             in_specs=[pl.BlockSpec(memory_space=pl.ANY)] * len(args),
             out_specs=pl.BlockSpec(memory_space=pltpu.VMEM),
             scratch_shapes=[pltpu.VMEM(a.shape, a.dtype) for a in args]
@@ -298,6 +307,7 @@
                 pltpu.VMEM((BORDER, features), BF16),
                 pltpu.VMEM((BORDER, features), BF16),
                 pltpu.VMEM((BORDER, features), BF16),
+                pltpu.VMEM((BORDER, features), BF16),
                 pltpu.SemaphoreType.DMA((len(args),)),
                 pltpu.SemaphoreType.DMA((len(SLOTS),)),
                 pltpu.SemaphoreType.DMA((len(SLOTS),)),

time: 25.1 us -> 22.5 us (0.90)
  the two profiles are of different devices: /device:TPU:1 before, /device:TPU:32 now
where the time goes in v2:
time: 22.5 us; the launch traced here: 22.4 us
  Pallas kernels  21.8 us (97%)
  local copies, waits for them, and re-layouts  0.67 us (3%)
    pallas_call x1, Pallas kernels, local(): pl.pallas_call(functools.partial(kernel, n_lat, n_lon), out_shape=pltpu.V...  21.8 us
    unnamed x1, local copies, waits for them, and re-layouts  0.67 us

profile of v2, /device:TPU:32, one launch (start us, length us, event | category | flops | bytes accessed | tf_op | source)
XLA Modules:
  0.0 22.4 jit_solution(16563067189118733379)
XLA Ops:
  0.0 21.8 %shard_map.136 = bf16[160,512]{1,0:T(8,128)(2,1)S(1)} custom-call(bf16[1024,512]{1,0:T(8,128)(2,1)} %bitcast.10, bf16[160,512]{1,0:T(8,128)(2,1)} %bitcast.11, f32[4,2048]{1,0:T(4,128)} %bitcast.12, s32[1,2048]{1,0:T(1,128)} %bitcast.13, s32[1,2048]{1,0:T(1,128)} %bitcast.14, bf16[512,512]{1,0:T(8,128)(2,1)} %wg_h.1, bf16[512,512]{1,0:T(8,128)(2,1)} %wm_h.1, ...), custom_call_target="tpu_custom_call" | custom-call | tf_op jit(solution)/shard_map/pallas_call | solution.py:293
  21.8 0.7 %copy.16 = bf16[1,1,160,512]{3,2,1,0:T(8,128)(2,1)} copy(bf16[1,1,160,512]{3,2,1,0:T(8,128)(2,1)S(1)} %bitcast.9) | data formatting | bytes 327680

commit v3 on v2

--- a/solution.py
+++ b/solution.py
@@ -10,7 +10,7 @@
 B_SIDE = 16
 BORDER = 8 * B_SIDE
 BLOCK = 512
-TAIL_BLOCK = 256
+TAIL_BLOCK = 512
 F32 = jnp.float32
 BF16 = jnp.bfloat16
 SLOTS = (3, 5, 0, 2, 6, 8, 1, 7)
@@ -21,17 +21,12 @@
     return jnp.where(codes == picks, jnp.ones((), BF16), jnp.zeros((), BF16))
 
 
-def silu(x):
-    half = 0.5 * x
+def silu_of_double(half):
     return half + half * jnp.tanh(half)
 
 
 def dot(a, b):
     return jnp.dot(a, b, preferred_element_type=F32)
-
-
-def dot_nt(a, b):
-    return lax.dot_general(a, b, (((1,), (1,)), ((), ())), preferred_element_type=F32)
 
 
 def pieces(x):
@@ -80,7 +75,7 @@
     border_v,
     pre_v,
     hid_v,
-    proj_v,
+    near_pick_v,
     near_v,
     part_v,
     arrived_v,
@@ -95,7 +90,7 @@
     rows = mesh_v.shape[0]
     features = mesh_v.shape[1]
     grid_rows = grid_v.shape[0]
-    edges = snd_v.shape[1]
+    edges = geo_v.shape[1]
     mesh_ids = pl.DeviceIdType.MESH
 
     def peer(slot, sign):
@@ -111,15 +106,15 @@
         else:
             pl.when(lat < n_lat - 1)(action)
 
-    def exchange(source, target, send_sem, recv_sem, sign):
+    def exchange(source, start, target, send_sem, recv_sem, sign):
         copies = []
         for slot in SLOTS:
             k = slot if slot < 4 else slot - 1
-            part = pl.ds(k * B_SIDE, CORNER_ROWS if slot % 2 == 0 else B_SIDE)
+            count = CORNER_ROWS if slot % 2 == 0 else B_SIDE
             copies.append(
                 pltpu.make_async_remote_copy(
-                    src_ref=source.at[part],
-                    dst_ref=target.at[part],
+                    src_ref=source.at[pl.ds(start + k * B_SIDE, count)],
+                    dst_ref=target.at[pl.ds(k * B_SIDE, count)],
                     send_sem=send_sem.at[k],
                     recv_sem=recv_sem.at[k],
                     device_id=peer(slot, sign),
@@ -128,8 +123,17 @@
             )
         return copies
 
-    near_v[...] = jnp.zeros_like(near_v)
-    arrived_v[...] = jnp.zeros_like(arrived_v)
+    def clear(slots, first, count):
+        for slot in slots:
+            k = slot if slot < 4 else slot - 1
+            here = pl.ds(k * B_SIDE + first, count)
+            near_v[here, :] = jnp.zeros((count, features), BF16)
+            arrived_v[here, :] = jnp.zeros((count, features), BF16)
+
+    clear((0, 2, 6, 8), CORNER_ROWS, B_SIDE - CORNER_ROWS)
+    pl.when(jnp.logical_or(lat == 0, lat == n_lat - 1))(
+        lambda: clear((0, 1, 2, 6, 7, 8), 0, B_SIDE)
+    )
     barrier = pltpu.get_barrier_semaphore()
     for slot in SLOTS:
         if_peer(
@@ -163,73 +167,71 @@
     gx_v[...] = jnp.zeros_like(gx_v)
     for name in ("mesh", "wm"):
         loads[name].wait()
-    proj_v[...] = dot(mesh_v[0:BORDER, :], wm_v[...]).astype(BF16)
-    own_t = dot_nt(wm_v[...].T, mesh_v[...])
+    own_at = pl.ds(grid_rows, rows)
+    table_v[own_at, :] = (0.5 * dot(mesh_v[...], wm_v[...])).astype(BF16)
+    loads["wg"].wait()
+    loads["grid"].wait()
+    for at in range(0, grid_rows, 512):
+        table_v[at : at + 512, :] = (
+            0.5 * dot(grid_v[at : at + 512, :], wg_v[...])
+        ).astype(BF16)
+    ends = jnp.where(jnp.logical_or(lat == 0, lat == n_lat - 1), 3, 0)
+    pl.semaphore_wait(barrier, len(SLOTS) - ends)
+    first = exchange(table_v, grid_rows, near_v, send1, recv1, -1)
+    for slot, copy in zip(SLOTS, first):
+        if_peer(slot, -1, copy.start)
     for name in ("we", "eb", "geo", "snd", "rcv"):
         loads[name].wait()
-
     w1, w2, w3 = pieces(we_v[...])
     g1, g2, g3 = pieces(geo_v[...])
     base = rows - 128
     for i, (g, w) in enumerate(((g1, w1), (g1, w2), (g2, w1), (g2, w2), (g1, w3), (g3, w1))):
-        gx_v[4 * i : 4 * i + 4, :] = g
-        extra_v[base + 4 * i : base + 4 * i + 4, :] = w
-    gx_v[24:27, :] = jnp.ones((3, edges), F32)
+        gx_v[base + 4 * i : base + 4 * i + 4, :] = g
+        extra_v[4 * i : 4 * i + 4, :] = w
+    gx_v[base + 24 : base + 27, :] = jnp.ones((3, edges), F32)
     for i, b in enumerate(pieces(eb_v[...])):
-        extra_v[base + 24 + i : base + 25 + i, :] = b
-    own_t = jnp.concatenate([own_t, jnp.zeros((features, 256 - rows), F32)], axis=1)
-    own_t = own_t + jnp.concatenate([jnp.zeros((features, 128), F32), extra_v[...].T], axis=1)
-    table_v[:, grid_rows : grid_rows + 256] = own_t.astype(BF16)
-    ends = jnp.where(jnp.logical_or(lat == 0, lat == n_lat - 1), 3, 0)
-    pl.semaphore_wait(barrier, len(SLOTS) - ends)
-    first = exchange(proj_v, near_v, send1, recv1, -1)
-    for slot, copy in zip(SLOTS, first):
-        if_peer(slot, -1, copy.start)
-    loads["wg"].wait()
-    loads["grid"].wait()
-    wg_t = wg_v[...].T
-    for at in range(0, grid_rows, 256):
-        table_v[:, at : at + 256] = dot_nt(wg_t, grid_v[at : at + 256, :]).astype(BF16)
+        extra_v[24 + i : 25 + i, :] = b
+    table_v[grid_rows + rows :, :] = (0.5 * extra_v[...]).astype(BF16)
     i16 = jnp.int16
-    grid_codes = lax.broadcasted_iota(jnp.int32, (grid_rows, BLOCK), 0).astype(i16)
-    own_codes = (lax.broadcasted_iota(jnp.int32, (rows, BLOCK), 0) + 4 * rows).astype(i16)
-    q = lax.broadcasted_iota(jnp.int32, (BORDER, BLOCK), 0)
+    snd_t = snd_v[...].T
+    rcv_t = rcv_v[...].T
+    lane = lax.broadcasted_iota(jnp.int32, (128, 128), 1)
+    own_codes = (lax.broadcasted_iota(jnp.int32, (rows, 128), 0) + 4 * rows).astype(i16)
+    q = lax.broadcasted_iota(jnp.int32, (BORDER, 128), 0)
     border_codes = (q + rows * ((q >> 4) + (q >= 64).astype(jnp.int32))).astype(i16)
+    lane_codes = (lane + rows * ((lane >> 4) + (lane >= 64).astype(jnp.int32))).astype(i16)
     for at in range(0, edges, BLOCK):
-        here = pl.ds(at, BLOCK)
-        snd = snd_v[:, here].astype(i16)
-        rcv = rcv_v[:, here].astype(i16)
-        own = onehot(own_codes, rcv)
-        own_v[:, here] = own
-        border_v[:, here] = onehot(border_codes, rcv)
-        stacked = jnp.concatenate(
-            [
-                onehot(grid_codes, snd),
-                own,
-                gx_v[:, here].astype(BF16),
-                jnp.zeros((256 - rows - 32, BLOCK), BF16),
-            ],
-            axis=0,
-        )
-        pre_v[:, here] = dot(table_v[...], stacked)
+        parts = []
+        for c in range(at // 128, (at + BLOCK) // 128):
+            here = pl.ds(c * 128, 128)
+            snd = jnp.broadcast_to(snd_t[:, c : c + 1], (128, 128)).astype(i16)
+            rcv = jnp.broadcast_to(rcv_t[:, c : c + 1], (128, 128)).astype(i16)
+            near_pick_v[here, :] = onehot(lane_codes, rcv)
+            rcv_row = rcv_v[c : c + 1, :].astype(i16)
+            own_v[:, here] = onehot(own_codes, rcv_row)
+            border_v[:, here] = onehot(border_codes, rcv_row)
+            columns = [
+                onehot((lane + t).astype(i16), snd) for t in range(0, grid_rows, 128)
+            ]
+            columns.append(onehot((lane + 4 * rows).astype(i16), rcv))
+            tail = jnp.where(lane < rows - 128, lane + 4 * rows + 128, -1).astype(i16)
+            columns.append(onehot(tail, rcv) + gx_v[:, here].astype(BF16).T)
+            parts.append(jnp.concatenate(columns, axis=1))
+        pre_v[pl.ds(at, BLOCK), :] = dot(jnp.concatenate(parts, axis=0), table_v[...])
     for slot, copy in zip(SLOTS, first):
         if_peer(slot, 1, copy.wait_recv)
-    near_t = near_v[...].T
-    part_sum = jnp.zeros((BORDER, features), F32)
-    ahead = dot(near_t, border_v[:, 0:TAIL_BLOCK])
+    ahead = dot(near_pick_v[0:TAIL_BLOCK, :], near_v[...])
     for at in range(0, edges, TAIL_BLOCK):
         here = pl.ds(at, TAIL_BLOCK)
-        full = pre_v[:, here] + ahead
+        full = pre_v[here, :] + ahead
         if at + TAIL_BLOCK < edges:
-            ahead = dot(near_t, border_v[:, at + TAIL_BLOCK : at + 2 * TAIL_BLOCK])
-        hidden = silu(full).astype(BF16)
-        hid_v[:, here] = hidden
-        part_sum = part_sum + dot_nt(border_v[:, here], hidden)
-    part_v[...] = part_sum.astype(BF16)
-    second = exchange(part_v, arrived_v, send2, recv2, 1)
+            ahead = dot(near_pick_v[at + TAIL_BLOCK : at + 2 * TAIL_BLOCK, :], near_v[...])
+        hid_v[here, :] = silu_of_double(full).astype(BF16)
+    part_v[...] = dot(border_v[...], hid_v[...]).astype(BF16)
+    second = exchange(part_v, 0, arrived_v, send2, recv2, 1)
     for slot, copy in zip(SLOTS, second):
         if_peer(slot, 1, copy.start)
-    own_sum = dot_nt(own_v[...], hid_v[...])
+    own_sum = dot(own_v[...], hid_v[...])
     for name in ("wnode", "wmsg", "wout", "gain", "nb"):
         loads[name].wait()
     joined = dot(wmsg_v[...], wnode_v[features : 2 * features, :]).astype(BF16)
@@ -242,7 +244,7 @@
         [own_sum[:BORDER] + arrived_v[...].astype(F32), own_sum[BORDER:]], axis=0
     )
     node_pre = node_pre + dot(total.astype(BF16), joined)
-    update = dot(silu(node_pre).astype(BF16), wout_v[...])
+    update = dot(silu_of_double(0.5 * node_pre).astype(BF16), wout_v[...])
     mean = jnp.mean(update, axis=-1, keepdims=True)
     centered = update - mean
     var = jnp.mean(centered * centered, axis=-1, keepdims=True)
@@ -275,8 +277,8 @@
             grid_latent[0, 0],
             mesh_latent[0, 0],
             edge_geometry[0, 0],
-            senders[0],
-            receivers[0],
+            senders[0, 0].reshape(-1, 128),
+            receivers[0, 0].reshape(-1, 128),
             w_grid,
             w_mesh,
             w_edge,
@@ -297,14 +299,14 @@
             out_specs=pl.BlockSpec(memory_space=pltpu.VMEM),
             scratch_shapes=[pltpu.VMEM(a.shape, a.dtype) for a in args]
             + [
-                pltpu.VMEM((features, grid_rows + 256), BF16),
-                pltpu.VMEM((128, features), F32),
-                pltpu.VMEM((32, edges), F32),
+                pltpu.VMEM((grid_rows + 256, features), BF16),
+                pltpu.VMEM((256 - rows, features), F32),
+                pltpu.VMEM((128, edges), F32),
                 pltpu.VMEM((rows, edges), BF16),
                 pltpu.VMEM((BORDER, edges), BF16),
-                pltpu.VMEM((features, edges), F32),
-                pltpu.VMEM((features, edges), BF16),
-                pltpu.VMEM((BORDER, features), BF16),
+                pltpu.VMEM((edges, features), F32),
+                pltpu.VMEM((edges, features), BF16),
+                pltpu.VMEM((edges, BORDER), BF16),
                 pltpu.VMEM((BORDER, features), BF16),
                 pltpu.VMEM((BORDER, features), BF16),
                 pltpu.VMEM((BORDER, features), BF16),

time: 22.5 us -> 21.3 us (0.947)
  Pallas kernels: 21.8 us -> 20.6 us
    pallas_call x1, Pallas kernels: 21.8 us -> 20.6 us  [local(): pl.pallas_call(functools.partial(kernel, n_lat, n_lon), out_shape=pltpu.V...]
where the time goes in v3:
time: 21.3 us; the launch traced here: 21.2 us
  Pallas kernels  20.6 us (97%)
  local copies, waits for them, and re-layouts  0.67 us (3%)
    pallas_call x1, Pallas kernels, local(): pl.pallas_call(functools.partial(kernel, n_lat, n_lon), out_shape=pltpu.V...  20.6 us
    unnamed x1, local copies, waits for them, and re-layouts  0.67 us

profile of v3, /device:TPU:32, one launch (start us, length us, event | category | flops | bytes accessed | tf_op | source)
XLA Modules:
  0.0 21.2 jit_solution(1484240628706148362)
XLA Ops:
  0.0 20.6 %shard_map.136 = bf16[160,512]{1,0:T(8,128)(2,1)S(1)} custom-call(bf16[1024,512]{1,0:T(8,128)(2,1)} %bitcast.10, bf16[160,512]{1,0:T(8,128)(2,1)} %bitcast.11, f32[4,2048]{1,0:T(4,128)} %bitcast.12, s32[16,128]{1,0:T(8,128)} %bitcast.13, s32[16,128]{1,0:T(8,128)} %bitcast.14, bf16[512,512]{1,0:T(8,128)(2,1)} %wg_h.1, bf16[512,512]{1,0:T(8,128)(2,1)} %wm_h.1, ...), custom_call_target="tpu_custom_call" | custom-call | tf_op jit(solution)/shard_map/pallas_call | solution.py:295
  20.6 0.7 %copy.16 = bf16[1,1,160,512]{3,2,1,0:T(8,128)(2,1)} copy(bf16[1,1,160,512]{3,2,1,0:T(8,128)(2,1)S(1)} %bitcast.9) | data formatting | bytes 327680
